TPU v7x, 32 devices: a whole 2x2x4 slice. The times are simulated.
32 devices in a mesh: blk: 8 (over z, x), bfly: 4 (over y, core).
Axes of the slice: x: 2, y: 2, z: 4, core: 2. Of those that a mesh axis runs over, the one named last changes fastest.
Arguments:
- port_vectors: bfloat16 [8, 4, 768, 128], P('blk', 'bfly'), may hold values from -6 to 6
- column_leaf: bfloat16 [8, 4, 384, 768], P('blk', 'bfly'), may hold values from -0.21875 to 0.21875
- transfer: bfloat16 [8, 4, 4, 384, 768], P('blk', None, 'bfly'), may hold values from -0.21875 to 0.21875
- row_leaf: bfloat16 [8, 4, 768, 384], P('blk', 'bfly'), may hold values from -0.3125 to 0.3125
Outputs:
- field: bfloat16 [4, 768, 128], P('bfly', 'blk')
All inputs are finite; a program needn't handle non-finite values.
Results may differ from a plain program's by a relative error of at most 0.0095.
Values may be sent and summed in bfloat16 or wider, within the bound.
A program may use at most 64 MiB of HBM per device.

v0:
```python
import functools
import math

import jax
import jax.numpy as jnp
from jax import lax
from jax.experimental import pallas as pl
from jax.experimental.pallas import tpu as pltpu
from jax.sharding import PartitionSpec as P

PIECES = 2
MESH = pl.DeviceIdType.MESH


def kernel(
    n_blk, n_bfly, pieces,
    ports_hbm, column_hbm, transfer_hbm, row_hbm, out_ref,
    ports, column, transfer, row, stacked, outgoing, incoming, merged, partial,
    load_sem, send_sem, recv_sem, scatter_sem, gather_sem,
):
    levels, rank, _ = transfer.shape
    owned = outgoing.shape[1]
    bit_count = n_bfly.bit_length() - 1
    block = lax.axis_index("blk")
    position = lax.axis_index("bfly")

    loads = [
        pltpu.make_async_copy(ports_hbm.at[0, 0], ports, load_sem.at[0]),
        pltpu.make_async_copy(column_hbm.at[0, 0], column, load_sem.at[1]),
    ]
    for level in range(levels):
        loads.append(
            pltpu.make_async_copy(
                transfer_hbm.at[0, level, 0], transfer.at[level], load_sem.at[2 + level]
            )
        )
    loads.append(pltpu.make_async_copy(row_hbm.at[0, 0], row, load_sem.at[2 + levels]))
    for load in loads:
        load.start()

    bits = [(position // 2**bit) % 2 for bit in range(bit_count)]
    partners = [position + (1 - 2 * bits[bit]) * 2**bit for bit in range(bit_count)]
    barrier = pltpu.get_barrier_semaphore()
    for bit in range(min(bit_count, levels)):
        pl.semaphore_signal(
            barrier, inc=1, device_id={"bfly": partners[bit]}, device_id_type=MESH
        )
    for step in range(1, n_blk):
        pl.semaphore_signal(
            barrier, inc=1, device_id={"blk": lax.rem(block + step, n_blk)}, device_id_type=MESH
        )

    loads[0].wait()
    loads[1].wait()
    state = jnp.dot(column[...], ports[...], preferred_element_type=jnp.float32)
    pl.semaphore_wait(barrier, min(bit_count, levels) + n_blk - 1)

    sends = []
    width = ports.shape[1] // pieces
    spans = [pl.ds(piece * width, width) for piece in range(pieces)]

    def side(which):
        return pl.ds(pl.multiple_of(which * rank, rank), rank)

    def send(level, piece, value):
        mine = bits[level % bit_count]
        stacked[level, mine, spans[piece], :] = value.astype(jnp.bfloat16)
        copy = pltpu.make_async_remote_copy(
            src_ref=stacked.at[level, mine, spans[piece], :],
            dst_ref=stacked.at[level, mine, spans[piece], :],
            send_sem=send_sem.at[level, piece],
            recv_sem=recv_sem.at[level, piece],
            device_id={"bfly": partners[level % bit_count]},
            device_id_type=MESH,
        )
        copy.start()
        sends.append(copy)
        return copy

    def mix(level, which, piece):
        return lax.dot_general(
            stacked[level, which, spans[piece], :], transfer[level, :, side(which)],
            (((1,), (1,)), ((), ())), preferred_element_type=jnp.float32,
        )

    def rows(which):
        return lax.dot_general(
            merged[:, side(which)], stacked[levels - 1, which],
            (((1,), (1,)), ((), ())), preferred_element_type=jnp.float32,
        )

    first = state.T
    flying = [
        send(0, piece, first[piece * width : (piece + 1) * width]) for piece in range(pieces)
    ]
    for level in range(levels - 1):
        mine = bits[level % bit_count]
        if level == 0:
            loads[2].wait()
            begun = [mix(0, mine, piece) for piece in range(pieces)]
        loads[3 + level].wait()
        following, later = [], []
        for piece in range(pieces):
            flying[piece].wait_recv()
            mixed = begun[piece] + mix(level, 1 - mine, piece)
            following.append(send(level + 1, piece, mixed))
            if level + 1 < levels - 1:
                later.append(mix(level + 1, bits[(level + 1) % bit_count], piece))
        flying, begun = following, later
        if level == min(1, levels - 2):
            loads[2 + levels].wait()
    level = levels - 1
    mine = bits[level % bit_count]
    merged[...] = jnp.dot(
        row[...], transfer[level], preferred_element_type=jnp.float32
    ).astype(jnp.bfloat16)
    partial[...] = rows(mine)
    for copy in flying:
        copy.wait_recv()
    total = partial[...] + rows(1 - mine)
    for index in range(n_blk):
        outgoing[index] = total[index * owned : (index + 1) * owned].astype(jnp.bfloat16)
    for step in range(1, n_blk):
        target = lax.rem(block + step, n_blk)
        copy = pltpu.make_async_remote_copy(
            src_ref=outgoing.at[target],
            dst_ref=incoming.at[step],
            send_sem=scatter_sem.at[step],
            recv_sem=gather_sem.at[step],
            device_id={"blk": target},
            device_id_type=MESH,
        )
        copy.start()
        sends.append(copy)
    total = outgoing[block].astype(jnp.float32)
    for step in range(1, n_blk):
        sends[levels * pieces + step - 1].wait_recv()
        total = total + incoming[step].astype(jnp.float32)
    out_ref[0] = (total * (1.0 / math.sqrt(n_blk))).astype(jnp.bfloat16)
    for copy in sends:
        copy.wait_send()


def solution(mesh):
    n_blk, n_bfly = mesh.shape["blk"], mesh.shape["bfly"]

    def local(port_vectors, column_leaf, transfer, row_leaf):
        _, _, leaf, ports = port_vectors.shape
        rank = column_leaf.shape[2]
        levels = transfer.shape[1]
        owned = row_leaf.shape[2] // n_blk
        bf16 = jnp.bfloat16
        return pl.pallas_call(
            functools.partial(kernel, n_blk, n_bfly, PIECES),
            out_shape=pltpu.VMEM((1, owned, ports), bf16),
            in_specs=[pl.BlockSpec(memory_space=pl.ANY)] * 4,
            out_specs=pl.BlockSpec(memory_space=pltpu.VMEM),
            scratch_shapes=[
                pltpu.VMEM((leaf, ports), bf16),
                pltpu.VMEM((rank, leaf), bf16),
                pltpu.VMEM((levels, rank, 2 * rank), bf16),
                pltpu.VMEM((row_leaf.shape[2], rank), bf16),
                pltpu.VMEM((levels, 2, ports, rank), bf16),
                pltpu.VMEM((n_blk, owned, ports), bf16),
                pltpu.VMEM((n_blk, owned, ports), bf16),
                pltpu.VMEM((row_leaf.shape[2], 2 * rank), bf16),
                pltpu.VMEM((row_leaf.shape[2], ports), jnp.float32),
                pltpu.SemaphoreType.DMA((3 + levels,)),
                pltpu.SemaphoreType.DMA((levels, PIECES)),
                pltpu.SemaphoreType.DMA((levels, PIECES)),
                pltpu.SemaphoreType.DMA((n_blk,)),
                pltpu.SemaphoreType.DMA((n_blk,)),
            ],
            compiler_params=pltpu.CompilerParams(collective_id=0, has_side_effects=True),
        )(port_vectors, column_leaf, transfer, row_leaf)

    placed = (
        P("blk", "bfly", None, None),
        P("blk", "bfly", None, None),
        P("blk", None, "bfly", None, None),
        P("blk", "bfly", None, None),
    )
    return jax.shard_map(
        local, mesh=mesh, in_specs=placed, out_specs=P("bfly", "blk", None), check_vma=False
    )
```

profile of v0, /device:TPU:0, one launch (start us, length us, event | category | flops | bytes accessed | tf_op | source)
XLA Modules:
  0.0 22.1 jit_solution(2216621216480003046)
XLA Ops:
  0.0 21.5 %shard_map.46 = bf16[1,96,128]{2,1,0:T(8,128)(2,1)S(1)} custom-call(bf16[1,1,768,128]{3,2,1,0:T(8,128)(2,1)} %ports_hbm.1, bf16[1,1,384,768]{3,2,1,0:T(8,128)(2,1)} %column_hbm.1, bf16[1,4,1,384,768]{4,3,2,1,0:T(8,128)(2,1)} %transfer_hbm.1, bf16[1,1,768,384]{3,2,1,0:T(8,128)(2,1)} %row_hbm.1), custom_call_target="tpu_custom_call" | custom-call | tf_op jit(solution)/shard_map/pallas_call | solution.py:153
  21.5 0.6 %copy.6 = bf16[1,96,128]{2,1,0:T(8,128)(2,1)} copy(bf16[1,96,128]{2,1,0:T(8,128)(2,1)S(1)} %shard_map.46) | data formatting | bytes 49152
where the time goes:
time: 22.3 us; the launch traced here: 22.1 us
  Pallas kernels  21.5 us (96%)
  local copies, waits for them, and re-layouts  0.61 us (3%)
    pallas_call x1, Pallas kernels, local(): pl.pallas_call(functools.partial(kernel, n_blk, n_bfly, PIECES), out_shap...  21.5 us
    unnamed x1, local copies, waits for them, and re-layouts  0.61 us

commit v1 on v0

v1 whole, which is shorter than its diff:
```python
import functools
import math

import jax
import jax.numpy as jnp
from jax import lax
from jax.experimental import pallas as pl
from jax.experimental.pallas import tpu as pltpu
from jax.sharding import PartitionSpec as P

PIECES = 2
MESH = pl.DeviceIdType.MESH
F32 = jnp.float32
BF16 = jnp.bfloat16


def plan(levels, bit_count):
    bits = [level % bit_count for level in range(levels)]
    stages, level = [], 1
    while level < levels - 1:
        assert bits[level] > 0
        pair = level + 1 < levels - 1 and bits[level + 1] == 0
        stages.append((level, level + 1) if pair else (level,))
        level += len(stages[-1])
    assert stages and bits[levels - 1] > 0
    return bits, stages


def contract(left, right):
    return lax.dot_general(left, right, (((1,), (1,)), ((), ())), preferred_element_type=F32)


def kernel(
    n_blk, n_bfly, pieces,
    ports_hbm, column_hbm, transfer_hbm, row_hbm, out_ref,
    ports, column, transfer, foreign, row, first, held, arrived, begun, turned, mixing, lent,
    last, outgoing, incoming, merged, partial,
    load_sem, row_sem, first_sem, weight_send, weight_recv, held_sem,
    stage_send, stage_recv, last_send, last_recv, down_send, down_recv, scatter_send, scatter_recv,
):
    levels, rank, _ = transfer.shape
    count = ports.shape[1]
    leaf = row.shape[0]
    owned = leaf // n_blk
    bits, stages = plan(levels, n_bfly.bit_length() - 1)
    entry, final = stages[0][0], levels - 1
    block = lax.axis_index("blk")
    position = lax.axis_index("bfly")
    core = lax.rem(position, 2)
    host, helper = core == 1, core == 0
    width = count // pieces
    spans = [pl.ds(piece * width, width) for piece in range(pieces)]
    group = owned // pieces

    def load(source, target, sem):
        copy = pltpu.make_async_copy(source, target, sem)
        copy.start()
        return copy

    loads = [
        load(ports_hbm.at[0, 0], ports, load_sem.at[levels]),
        load(column_hbm.at[0, 0], column, load_sem.at[levels + 1]),
    ]
    transfer_loads = [
        load(transfer_hbm.at[0, level, 0], transfer.at[level], load_sem.at[level])
        for level in [0, 1, levels - 1] + list(range(2, levels - 1))
    ]
    transfer_loads = {
        level: copy
        for level, copy in zip([0, 1, levels - 1] + list(range(2, levels - 1)), transfer_loads)
    }
    row_loads = []
    for slot in range(n_blk):
        owner = block ^ (n_blk - 1 - slot)
        row_loads.append(
            load(
                row_hbm.at[0, 0, pl.ds(pl.multiple_of(owner * owned, owned), owned)],
                row.at[pl.ds(slot * owned, owned)],
                row_sem.at[slot],
            )
        )

    def side(which):
        return pl.ds(pl.multiple_of(which * rank, rank), rank)

    def bit_of(level):
        return lax.rem(position // 2 ** bits[level], 2)

    def across(level, to_core):
        place = position + (1 - 2 * bit_of(level)) * 2 ** bits[level]
        return {"bfly": place - core + to_core}

    mate = {"bfly": position + 1 - 2 * core}
    barrier = pltpu.get_barrier_semaphore()

    def greet(target):
        pl.semaphore_signal(barrier, inc=1, device_id=target, device_id_type=MESH)

    host_bits = {}
    for level in [stage[0] for stage in stages] + [final]:
        host_bits.setdefault(bits[level], level)
    mixed_bits = {bits[final]: final, bits[entry]: entry}
    greet(mate)
    for level in mixed_bits.values():
        greet(across(level, 1 - core))

    @pl.when(host)
    def _():
        for level in host_bits.values():
            greet(across(level, 1))

    for step in range(1, n_blk):
        greet({"blk": block ^ step})

    def remote(source, target, send_sem, recv_sem, device):
        return pltpu.make_async_remote_copy(
            src_ref=source, dst_ref=target, send_sem=send_sem, recv_sem=recv_sem,
            device_id=device, device_id_type=MESH,
        )

    first_copy = remote(first.at[core], first.at[core], first_sem.at[0], first_sem.at[1], mate)
    weight_copies = [
        remote(
            transfer.at[1 + index], foreign.at[index], weight_send.at[index], weight_recv.at[index], mate
        )
        for index in range(levels - 2)
    ]
    held_copy = remote(held.at[0, 0], held.at[0, 0], held_sem.at[0], held_sem.at[1], mate)

    def stage_copy(index, which, piece):
        return remote(
            held.at[index, which, spans[piece]], arrived.at[index, which, spans[piece]],
            stage_send.at[index, which, piece], stage_recv.at[index, which, piece],
            across(stages[index][0], 1),
        )

    mine = bit_of(final)

    def last_copy(which, piece):
        source = lent.at[spans[piece]] if which == 0 else last.at[mine, spans[piece]]
        return remote(
            source, last.at[mine, spans[piece]], last_send.at[which, piece], last_recv.at[piece],
            across(final, which),
        )

    def down_copy(piece):
        return remote(
            lent.at[spans[piece]], last.at[mine, spans[piece]], down_send.at[piece],
            down_recv.at[piece], mate,
        )

    def scatter_copy(piece, slot):
        return remote(
            outgoing.at[piece, slot], incoming.at[piece, slot],
            scatter_send.at[piece, slot], scatter_recv.at[piece, slot],
            {"blk": block ^ (n_blk - 1 - slot)},
        )

    def rows(which, piece):
        value = last[which, spans[piece], :]
        return contract(merged[:, side(which)], jnp.concatenate([value] * pieces, axis=0))

    loads[0].wait()
    loads[1].wait()
    state = jnp.dot(column[...], ports[...], preferred_element_type=F32)
    first[core] = state.T.astype(BF16)
    pl.semaphore_wait(barrier, len(mixed_bits) + n_blk + core * len(host_bits))
    first_copy.start()
    transfer_loads[1].wait()

    @pl.when(helper)
    def _():
        weight_copies[0].start()

    transfer_loads[0].wait()
    own = contract(first[core], transfer[0, :, side(core)])
    transfer_loads[final].wait()
    for copy in row_loads:
        copy.wait()
    merged[...] = jnp.dot(row[...], transfer[final], preferred_element_type=F32).astype(BF16)
    first_copy.wait_recv()
    state = own + contract(first[1 - core], transfer[0, :, side(1 - core)])
    held[0, core] = state.astype(BF16)
    for piece in range(pieces):
        stage_copy(0, core, piece).start()
    for level in range(2, final):
        transfer_loads[level].wait()

    @pl.when(helper)
    def _():
        held_copy.start()
        for copy in weight_copies[1:]:
            copy.start()
        for piece in range(pieces):
            down_copy(piece).wait_recv()
            partial[piece] = rows(mine, piece)

    def weights(level, which):
        return transfer.at[level] if which else foreign.at[level - 1]

    def mix(index, states, incoming_side):
        stage = stages[index]
        if len(stage) == 2:
            joined = jnp.concatenate(states, axis=1)
            return jnp.dot(joined, mixing[incoming_side], preferred_element_type=F32)
        which = bit_of(stage[0]) if incoming_side == 0 else 1 - bit_of(stage[0])
        return jnp.concatenate(
            [contract(states[c], weights(stage[0], c)[:, side(which)]) for c in range(2)], axis=1
        )

    def prepare(stage):
        low, high = stage
        bit = bit_of(low)
        for inner in (1, 0):
            if inner == 0:
                weight_copies[low - 1].wait_recv()
            for half, which in ((0, bit), (1, 1 - bit)):
                turned[inner, half] = weights(low, inner)[:, side(which)].T
                mixing[half, inner * rank : (inner + 1) * rank, rank:] = contract(
                    turned[inner, half], weights(high, 1)[:, inner * rank : (inner + 1) * rank]
                ).astype(BF16)
        weight_copies[high - 1].wait_recv()
        for inner in (0, 1):
            for half in range(2):
                mixing[half, inner * rank : (inner + 1) * rank, :rank] = contract(
                    turned[inner, half], weights(high, 0)[:, inner * rank : (inner + 1) * rank]
                ).astype(BF16)

    @pl.when(host)
    def _():
        for index, stage in enumerate(stages):
            if len(stage) == 2:
                prepare(stage)
            else:
                weight_copies[stage[0] - 1].wait_recv()
            if index == 0:
                held_copy.wait_recv()
            begun[...] = mix(index, [held[index, 0], held[index, 1]], 0)
            for piece in range(pieces):
                for which in range(2):
                    stage_copy(index, which, piece).wait_recv()
                total = begun[spans[piece], :] + mix(
                    index, [arrived[index, 0, spans[piece], :], arrived[index, 1, spans[piece], :]], 1
                )
                total = total.astype(BF16)
                if index + 1 < len(stages):
                    for which in range(2):
                        held[index + 1, which, spans[piece], :] = total[:, which * rank : (which + 1) * rank]
                        stage_copy(index + 1, which, piece).start()
                else:
                    lent[spans[piece], :] = total[:, :rank]
                    last_copy(0, piece).start()
                    last[mine, spans[piece], :] = total[:, rank:]
                    last_copy(1, piece).start()
                    down_copy(piece).start()
                    partial[piece] = rows(mine, piece)

    lane = lax.broadcasted_iota(jnp.int32, (group, count), 1)

    def choose(values):
        result = values[0]
        for k in range(1, pieces):
            result = jnp.where(lane < k * width, result, values[k])
        return result

    for piece in range(pieces):
        last_copy(1, piece).wait_recv()
        total = partial[piece] + rows(1 - mine, piece)
        for slot in range(n_blk):
            packed = choose(
                [
                    total[slot * owned + g * group : slot * owned + (g + 1) * group]
                    for g in ((k - piece) % pieces for k in range(pieces))
                ]
            )
            outgoing[piece, slot] = packed.astype(BF16)
            if slot < n_blk - 1:
                scatter_copy(piece, slot).start()

    sums = []
    for piece in range(pieces):
        total = outgoing[piece, n_blk - 1].astype(F32)
        for slot in range(n_blk - 2, -1, -1):
            scatter_copy(piece, slot).wait_recv()
            total = total + incoming[piece, slot].astype(F32)
        sums.append(total * (1.0 / math.sqrt(n_blk)))
    for g in range(pieces):
        value = choose([sums[(k - g) % pieces] for k in range(pieces)])
        if g:
            value = pltpu.roll(value, (count - g * width) % count, 1)
        out_ref[0, g * group : (g + 1) * group, :] = value.astype(BF16)

    first_copy.wait_send()
    for piece in range(pieces):
        stage_copy(0, core, piece).wait_send()
        for slot in range(n_blk - 1):
            scatter_copy(piece, slot).wait_send()

    @pl.when(helper)
    def _():
        held_copy.wait_send()
        for copy in weight_copies:
            copy.wait_send()

    @pl.when(host)
    def _():
        for piece in range(pieces):
            for index in range(1, len(stages)):
                for which in range(2):
                    stage_copy(index, which, piece).wait_send()
            last_copy(0, piece).wait_send()
            last_copy(1, piece).wait_send()
            down_copy(piece).wait_send()


def solution(mesh):
    n_blk, n_bfly = mesh.shape["blk"], mesh.shape["bfly"]

    def local(port_vectors, column_leaf, transfer, row_leaf):
        _, _, leaf, ports = port_vectors.shape
        rank = column_leaf.shape[2]
        levels = transfer.shape[1]
        rows = row_leaf.shape[2]
        owned = rows // n_blk
        _, stages = plan(levels, n_bfly.bit_length() - 1)
        assert n_blk & (n_blk - 1) == 0
        dma = pltpu.SemaphoreType.DMA
        return pl.pallas_call(
            functools.partial(kernel, n_blk, n_bfly, PIECES),
            out_shape=pltpu.VMEM((1, owned, ports), BF16),
            in_specs=[pl.BlockSpec(memory_space=pl.ANY)] * 4,
            out_specs=pl.BlockSpec(memory_space=pltpu.VMEM),
            scratch_shapes=[
                pltpu.VMEM((leaf, ports), BF16),
                pltpu.VMEM((rank, leaf), BF16),
                pltpu.VMEM((levels, rank, 2 * rank), BF16),
                pltpu.VMEM((levels - 2, rank, 2 * rank), BF16),
                pltpu.VMEM((rows, rank), BF16),
                pltpu.VMEM((2, ports, rank), BF16),
                pltpu.VMEM((len(stages), 2, ports, rank), BF16),
                pltpu.VMEM((len(stages), 2, ports, rank), BF16),
                pltpu.VMEM((ports, 2 * rank), F32),
                pltpu.VMEM((2, 2, rank, rank), BF16),
                pltpu.VMEM((2, 2 * rank, 2 * rank), BF16),
                pltpu.VMEM((ports, rank), BF16),
                pltpu.VMEM((2, ports, rank), BF16),
                pltpu.VMEM((PIECES, n_blk, owned // PIECES, ports), BF16),
                pltpu.VMEM((PIECES, n_blk, owned // PIECES, ports), BF16),
                pltpu.VMEM((rows, 2 * rank), BF16),
                pltpu.VMEM((PIECES, rows, ports), F32),
                dma((levels + 2,)),
                dma((n_blk,)),
                dma((2,)),
                dma((levels - 2,)),
                dma((levels - 2,)),
                dma((2,)),
                dma((len(stages), 2, PIECES)),
                dma((len(stages), 2, PIECES)),
                dma((2, PIECES)),
                dma((PIECES,)),
                dma((PIECES,)),
                dma((PIECES,)),
                dma((PIECES, n_blk)),
                dma((PIECES, n_blk)),
            ],
            compiler_params=pltpu.CompilerParams(collective_id=0, has_side_effects=True),
        )(port_vectors, column_leaf, transfer, row_leaf)

    placed = (
        P("blk", "bfly", None, None),
        P("blk", "bfly", None, None),
        P("blk", None, "bfly", None, None),
        P("blk", "bfly", None, None),
    )
    return jax.shard_map(
        local, mesh=mesh, in_specs=placed, out_specs=P("bfly", "blk", None), check_vma=False
    )
```

time: 22.3 us -> 21.8 us (0.978)
  Pallas kernels: 21.5 us -> 21.1 us
    pallas_call x1, Pallas kernels: 21.5 us -> 21.1 us  [local(): pl.pallas_call(functools.partial(kernel, n_blk, n_bfly, PIECES), out_shap...]
where the time goes in v1:
time: 21.8 us; the launch traced here: 21.7 us
  Pallas kernels  21.1 us (97%)
  local copies, waits for them, and re-layouts  0.61 us (3%)
    pallas_call x1, Pallas kernels, local(): pl.pallas_call(functools.partial(kernel, n_blk, n_bfly, PIECES), out_shap...  21.1 us
    unnamed x1, local copies, waits for them, and re-layouts  0.61 us

profile of v1, /device:TPU:0, one launch (start us, length us, event | category | flops | bytes accessed | tf_op | source)
XLA Modules:
  0.0 21.7 jit_solution(9158799441758654205)
XLA Ops:
  0.0 21.1 %shard_map.46 = bf16[1,96,128]{2,1,0:T(8,128)(2,1)S(1)} custom-call(bf16[1,1,768,128]{3,2,1,0:T(8,128)(2,1)} %ports_hbm.1, bf16[1,1,384,768]{3,2,1,0:T(8,128)(2,1)} %column_hbm.1, bf16[1,4,1,384,768]{4,3,2,1,0:T(8,128)(2,1)} %transfer_hbm.1, bf16[1,1,768,384]{3,2,1,0:T(8,128)(2,1)} %row_hbm.1), custom_call_target="tpu_custom_call" | custom-call | tf_op jit(solution)/shard_map/pallas_call | solution.py:328
  21.1 0.6 %copy.6 = bf16[1,96,128]{2,1,0:T(8,128)(2,1)} copy(bf16[1,96,128]{2,1,0:T(8,128)(2,1)S(1)} %shard_map.46) | data formatting | bytes 49152

commit v2 on v1

--- a/solution.py
+++ b/solution.py
@@ -37,6 +37,7 @@
     last, outgoing, incoming, merged, partial,
     load_sem, row_sem, first_sem, weight_send, weight_recv, held_sem,
     stage_send, stage_recv, last_send, last_recv, down_send, down_recv, scatter_send, scatter_recv,
+    meet_sem,
 ):
     levels, rank, _ = transfer.shape
     count = ports.shape[1]
@@ -109,8 +110,22 @@
         for level in host_bits.values():
             greet(across(level, 1))
 
-    for step in range(1, n_blk):
-        greet({"blk": block ^ step})
+    blk_bits = n_blk.bit_length() - 1
+    for bit in range(blk_bits):
+        greet({"blk": block ^ (1 << bit)})
+
+    def tell(turn):
+        if turn < blk_bits - 1:
+            for bit in range(blk_bits):
+                pl.semaphore_signal(
+                    meet_sem.at[turn, bit], inc=1, device_id={"blk": block ^ (1 << bit)},
+                    device_id_type=MESH,
+                )
+
+    def hear(turn):
+        if turn < blk_bits - 1:
+            for bit in range(blk_bits):
+                pl.semaphore_wait(meet_sem.at[turn, bit], 1)
 
     def remote(source, target, send_sem, recv_sem, device):
         return pltpu.make_async_remote_copy(
@@ -164,7 +179,8 @@
     loads[1].wait()
     state = jnp.dot(column[...], ports[...], preferred_element_type=F32)
     first[core] = state.T.astype(BF16)
-    pl.semaphore_wait(barrier, len(mixed_bits) + n_blk + core * len(host_bits))
+    pl.semaphore_wait(barrier, 1 + len(mixed_bits) + blk_bits + core * len(host_bits))
+    tell(0)
     first_copy.start()
     transfer_loads[1].wait()
 
@@ -183,6 +199,8 @@
     held[0, core] = state.astype(BF16)
     for piece in range(pieces):
         stage_copy(0, core, piece).start()
+    hear(0)
+    tell(1)
     for level in range(2, final):
         transfer_loads[level].wait()
 
@@ -255,6 +273,9 @@
                     down_copy(piece).start()
                     partial[piece] = rows(mine, piece)
 
+    for turn in range(1, blk_bits - 1):
+        hear(turn)
+        tell(turn + 1)
     lane = lax.broadcasted_iota(jnp.int32, (group, count), 1)
 
     def choose(values):
@@ -362,6 +383,7 @@
                 dma((PIECES,)),
                 dma((PIECES, n_blk)),
                 dma((PIECES, n_blk)),
+                pltpu.SemaphoreType.REGULAR((n_blk.bit_length(), n_blk.bit_length())),
             ],
             compiler_params=pltpu.CompilerParams(collective_id=0, has_side_effects=True),
         )(port_vectors, column_leaf, transfer, row_leaf)

time: 21.8 us -> 22 us (level)
  no operation moved by 1% of the time
where the time goes in v2:
time: 22 us; the launch traced here: 21.9 us
  Pallas kernels  21.2 us (96%)
  local copies, waits for them, and re-layouts  0.61 us (3%)
    pallas_call x1, Pallas kernels, local(): pl.pallas_call(functools.partial(kernel, n_blk, n_bfly, PIECES), out_shap...  21.2 us
    unnamed x1, local copies, waits for them, and re-layouts  0.61 us

profile of v2, /device:TPU:0, one launch (start us, length us, event | category | flops | bytes accessed | tf_op | source)
XLA Modules:
  0.0 21.9 jit_solution(786878772307704296)
XLA Ops:
  0.0 21.2 %shard_map.46 = bf16[1,96,128]{2,1,0:T(8,128)(2,1)S(1)} custom-call(bf16[1,1,768,128]{3,2,1,0:T(8,128)(2,1)} %ports_hbm.1, bf16[1,1,384,768]{3,2,1,0:T(8,128)(2,1)} %column_hbm.1, bf16[1,4,1,384,768]{4,3,2,1,0:T(8,128)(2,1)} %transfer_hbm.1, bf16[1,1,768,384]{3,2,1,0:T(8,128)(2,1)} %row_hbm.1), custom_call_target="tpu_custom_call" | custom-call | tf_op jit(solution)/shard_map/pallas_call | solution.py:349
  21.2 0.6 %copy.6 = bf16[1,96,128]{2,1,0:T(8,128)(2,1)} copy(bf16[1,96,128]{2,1,0:T(8,128)(2,1)S(1)} %shard_map.46) | data formatting | bytes 49152

commit v3 on v2

--- a/solution.py
+++ b/solution.py
@@ -8,7 +8,7 @@
 from jax.experimental.pallas import tpu as pltpu
 from jax.sharding import PartitionSpec as P
 
-PIECES = 2
+PIECES = 4
 MESH = pl.DeviceIdType.MESH
 F32 = jnp.float32
 BF16 = jnp.bfloat16
@@ -62,13 +62,9 @@
         load(ports_hbm.at[0, 0], ports, load_sem.at[levels]),
         load(column_hbm.at[0, 0], column, load_sem.at[levels + 1]),
     ]
-    transfer_loads = [
-        load(transfer_hbm.at[0, level, 0], transfer.at[level], load_sem.at[level])
-        for level in [0, 1, levels - 1] + list(range(2, levels - 1))
-    ]
     transfer_loads = {
-        level: copy
-        for level, copy in zip([0, 1, levels - 1] + list(range(2, levels - 1)), transfer_loads)
+        level: load(transfer_hbm.at[0, level, 0], transfer.at[level], load_sem.at[level])
+        for level in range(levels)
     }
     row_loads = []
     for slot in range(n_blk):
@@ -171,9 +167,38 @@
             {"blk": block ^ (n_blk - 1 - slot)},
         )
 
-    def rows(which, piece):
-        value = last[which, spans[piece], :]
-        return contract(merged[:, side(which)], jnp.concatenate([value] * pieces, axis=0))
+    def scatter(piece, target, held_back):
+        far = (block >= n_blk // 2) if n_blk // 4 <= target < n_blk // 2 else None
+        if held_back:
+            ready = far
+        elif far is None:
+            ready = block != target
+        else:
+            ready = jnp.logical_and(block != target, jnp.logical_not(far))
+
+        @pl.when(ready)
+        def _():
+            scatter_copy(piece, (n_blk - 1) - (block ^ target)).start()
+
+    def own_rows():
+        value = contract(merged[:, side(mine)], last[mine])
+        for slot in range(n_blk):
+            for g in range(pieces):
+                start = slot * owned + g * group
+                part = value[start : start + group]
+                partial[start : start + group, :] = pltpu.roll(part, g * width, 1) if g else part
+
+    def other_rows(piece):
+        value = last[1 - mine, spans[piece], :]
+        return contract(merged[:, side(1 - mine)], jnp.concatenate([value] * pieces, axis=0))
+
+    def weights(level, which):
+        return transfer.at[level] if which else foreign.at[level - 1]
+
+    def turn(level, inner):
+        bit = bit_of(level)
+        for half, which in ((0, bit), (1, 1 - bit)):
+            turned[inner, half * rank : (half + 1) * rank] = weights(level, inner)[:, side(which)].T
 
     loads[0].wait()
     loads[1].wait()
@@ -182,18 +207,25 @@
     pl.semaphore_wait(barrier, 1 + len(mixed_bits) + blk_bits + core * len(host_bits))
     tell(0)
     first_copy.start()
-    transfer_loads[1].wait()
+    for level in range(final):
+        transfer_loads[level].wait()
 
     @pl.when(helper)
     def _():
-        weight_copies[0].start()
-
-    transfer_loads[0].wait()
+        for copy in weight_copies:
+            copy.start()
+
     own = contract(first[core], transfer[0, :, side(core)])
     transfer_loads[final].wait()
     for copy in row_loads:
         copy.wait()
     merged[...] = jnp.dot(row[...], transfer[final], preferred_element_type=F32).astype(BF16)
+
+    @pl.when(host)
+    def _():
+        if len(stages[0]) == 2:
+            turn(entry, 1)
+
     first_copy.wait_recv()
     state = own + contract(first[1 - core], transfer[0, :, side(1 - core)])
     held[0, core] = state.astype(BF16)
@@ -201,20 +233,13 @@
         stage_copy(0, core, piece).start()
     hear(0)
     tell(1)
-    for level in range(2, final):
-        transfer_loads[level].wait()
 
     @pl.when(helper)
     def _():
         held_copy.start()
-        for copy in weight_copies[1:]:
-            copy.start()
         for piece in range(pieces):
             down_copy(piece).wait_recv()
-            partial[piece] = rows(mine, piece)
-
-    def weights(level, which):
-        return transfer.at[level] if which else foreign.at[level - 1]
+        own_rows()
 
     def mix(index, states, incoming_side):
         stage = stages[index]
@@ -226,28 +251,29 @@
             [contract(states[c], weights(stage[0], c)[:, side(which)]) for c in range(2)], axis=1
         )
 
+    def join(low, high, inner, outer):
+        both = contract(turned[inner], weights(high, outer)[:, inner * rank : (inner + 1) * rank])
+        for half in range(2):
+            mixing[half, inner * rank : (inner + 1) * rank, outer * rank : (outer + 1) * rank] = both[
+                half * rank : (half + 1) * rank
+            ].astype(BF16)
+
     def prepare(stage):
         low, high = stage
-        bit = bit_of(low)
-        for inner in (1, 0):
-            if inner == 0:
-                weight_copies[low - 1].wait_recv()
-            for half, which in ((0, bit), (1, 1 - bit)):
-                turned[inner, half] = weights(low, inner)[:, side(which)].T
-                mixing[half, inner * rank : (inner + 1) * rank, rank:] = contract(
-                    turned[inner, half], weights(high, 1)[:, inner * rank : (inner + 1) * rank]
-                ).astype(BF16)
+        join(low, high, 1, 1)
+        weight_copies[low - 1].wait_recv()
+        turn(low, 0)
+        join(low, high, 0, 1)
         weight_copies[high - 1].wait_recv()
-        for inner in (0, 1):
-            for half in range(2):
-                mixing[half, inner * rank : (inner + 1) * rank, :rank] = contract(
-                    turned[inner, half], weights(high, 0)[:, inner * rank : (inner + 1) * rank]
-                ).astype(BF16)
+        join(low, high, 1, 0)
+        join(low, high, 0, 0)
 
     @pl.when(host)
     def _():
         for index, stage in enumerate(stages):
             if len(stage) == 2:
+                if index:
+                    turn(stage[0], 1)
                 prepare(stage)
             else:
                 weight_copies[stage[0] - 1].wait_recv()
@@ -271,11 +297,11 @@
                     last[mine, spans[piece], :] = total[:, rank:]
                     last_copy(1, piece).start()
                     down_copy(piece).start()
-                    partial[piece] = rows(mine, piece)
-
-    for turn in range(1, blk_bits - 1):
-        hear(turn)
-        tell(turn + 1)
+        own_rows()
+
+    for hop in range(1, blk_bits - 1):
+        hear(hop)
+        tell(hop + 1)
     lane = lax.broadcasted_iota(jnp.int32, (group, count), 1)
 
     def choose(values):
@@ -286,7 +312,7 @@
 
     for piece in range(pieces):
         last_copy(1, piece).wait_recv()
-        total = partial[piece] + rows(1 - mine, piece)
+        total = partial[...] + other_rows(piece)
         for slot in range(n_blk):
             packed = choose(
                 [
@@ -295,11 +321,38 @@
                 ]
             )
             outgoing[piece, slot] = packed.astype(BF16)
-            if slot < n_blk - 1:
-                scatter_copy(piece, slot).start()
+        for target in range(n_blk):
+            scatter(piece, target, False)
+    for piece in range(pieces):
+        for target in range(n_blk // 4, n_blk // 2):
+            scatter(piece, target, True)
+
+    first_copy.wait_send()
+    for piece in range(pieces):
+        stage_copy(0, core, piece).wait_send()
+
+    @pl.when(helper)
+    def _():
+        held_copy.wait_send()
+        for copy in weight_copies:
+            copy.wait_send()
+
+    @pl.when(host)
+    def _():
+        for piece in range(pieces):
+            for index in range(1, len(stages)):
+                for which in range(2):
+                    stage_copy(index, which, piece).wait_send()
+            last_copy(0, piece).wait_send()
+            last_copy(1, piece).wait_send()
+            down_copy(piece).wait_send()
 
     sums = []
     for piece in range(pieces):
+        if piece == pieces - 1:
+            for other in range(pieces):
+                for slot in range(n_blk - 1):
+                    scatter_copy(other, slot).wait_send()
         total = outgoing[piece, n_blk - 1].astype(F32)
         for slot in range(n_blk - 2, -1, -1):
             scatter_copy(piece, slot).wait_recv()
@@ -310,28 +363,6 @@
         if g:
             value = pltpu.roll(value, (count - g * width) % count, 1)
         out_ref[0, g * group : (g + 1) * group, :] = value.astype(BF16)
-
-    first_copy.wait_send()
-    for piece in range(pieces):
-        stage_copy(0, core, piece).wait_send()
-        for slot in range(n_blk - 1):
-            scatter_copy(piece, slot).wait_send()
-
-    @pl.when(helper)
-    def _():
-        held_copy.wait_send()
-        for copy in weight_copies:
-            copy.wait_send()
-
-    @pl.when(host)
-    def _():
-        for piece in range(pieces):
-            for index in range(1, len(stages)):
-                for which in range(2):
-                    stage_copy(index, which, piece).wait_send()
-            last_copy(0, piece).wait_send()
-            last_copy(1, piece).wait_send()
-            down_copy(piece).wait_send()
 
 
 def solution(mesh):
@@ -361,14 +392,14 @@
                 pltpu.VMEM((len(stages), 2, ports, rank), BF16),
                 pltpu.VMEM((len(stages), 2, ports, rank), BF16),
                 pltpu.VMEM((ports, 2 * rank), F32),
-                pltpu.VMEM((2, 2, rank, rank), BF16),
+                pltpu.VMEM((2, 2 * rank, rank), BF16),
                 pltpu.VMEM((2, 2 * rank, 2 * rank), BF16),
                 pltpu.VMEM((ports, rank), BF16),
                 pltpu.VMEM((2, ports, rank), BF16),
                 pltpu.VMEM((PIECES, n_blk, owned // PIECES, ports), BF16),
                 pltpu.VMEM((PIECES, n_blk, owned // PIECES, ports), BF16),
                 pltpu.VMEM((rows, 2 * rank), BF16),
-                pltpu.VMEM((PIECES, rows, ports), F32),
+                pltpu.VMEM((rows, ports), F32),
                 dma((levels + 2,)),
                 dma((n_blk,)),
                 dma((2,)),

time: 22 us -> 21 us (0.955)
  Pallas kernels: 21.2 us -> 20.3 us
    pallas_call x1, Pallas kernels: 21.2 us -> 20.3 us  [local(): pl.pallas_call(functools.partial(kernel, n_blk, n_bfly, PIECES), out_shap...]
where the time goes in v3:
time: 21 us; the launch traced here: 20.9 us
  Pallas kernels  20.3 us (97%)
  local copies, waits for them, and re-layouts  0.61 us (3%)
    pallas_call x1, Pallas kernels, local(): pl.pallas_call(functools.partial(kernel, n_blk, n_bfly, PIECES), out_shap...  20.3 us
    unnamed x1, local copies, waits for them, and re-layouts  0.61 us

profile of v3, /device:TPU:0, one launch (start us, length us, event | category | flops | bytes accessed | tf_op | source)
XLA Modules:
  0.0 20.9 jit_solution(5901158771006990039)
XLA Ops:
  0.0 20.3 %shard_map.46 = bf16[1,96,128]{2,1,0:T(8,128)(2,1)S(1)} custom-call(bf16[1,1,768,128]{3,2,1,0:T(8,128)(2,1)} %ports_hbm.1, bf16[1,1,384,768]{3,2,1,0:T(8,128)(2,1)} %column_hbm.1, bf16[1,4,1,384,768]{4,3,2,1,0:T(8,128)(2,1)} %transfer_hbm.1, bf16[1,1,768,384]{3,2,1,0:T(8,128)(2,1)} %row_hbm.1), custom_call_target="tpu_custom_call" | custom-call | tf_op jit(solution)/shard_map/pallas_call | solution.py:380
  20.3 0.6 %copy.6 = bf16[1,96,128]{2,1,0:T(8,128)(2,1)} copy(bf16[1,96,128]{2,1,0:T(8,128)(2,1)S(1)} %shard_map.46) | data formatting | bytes 49152

commit v4 on v3

--- a/solution.py
+++ b/solution.py
@@ -35,9 +35,8 @@
     ports_hbm, column_hbm, transfer_hbm, row_hbm, out_ref,
     ports, column, transfer, foreign, row, first, held, arrived, begun, turned, mixing, lent,
     last, outgoing, incoming, merged, partial,
-    load_sem, row_sem, first_sem, weight_send, weight_recv, held_sem,
-    stage_send, stage_recv, last_send, last_recv, down_send, down_recv, scatter_send, scatter_recv,
-    meet_sem,
+    load_sem, first_sem, weight_sem, held_sem, stage_send, stage_recv, last_send, last_recv, down_sem,
+    scatter_send, scatter_recv, meet_sem,
 ):
     levels, rank, _ = transfer.shape
     count = ports.shape[1]
@@ -73,7 +72,7 @@
             load(
                 row_hbm.at[0, 0, pl.ds(pl.multiple_of(owner * owned, owned), owned)],
                 row.at[pl.ds(slot * owned, owned)],
-                row_sem.at[slot],
+                load_sem.at[levels + 2],
             )
         )
 
@@ -114,14 +113,12 @@
         if turn < blk_bits - 1:
             for bit in range(blk_bits):
                 pl.semaphore_signal(
-                    meet_sem.at[turn, bit], inc=1, device_id={"blk": block ^ (1 << bit)},
-                    device_id_type=MESH,
+                    meet_sem.at[turn], inc=1, device_id={"blk": block ^ (1 << bit)}, device_id_type=MESH
                 )
 
     def hear(turn):
         if turn < blk_bits - 1:
-            for bit in range(blk_bits):
-                pl.semaphore_wait(meet_sem.at[turn, bit], 1)
+            pl.semaphore_wait(meet_sem.at[turn], blk_bits)
 
     def remote(source, target, send_sem, recv_sem, device):
         return pltpu.make_async_remote_copy(
@@ -130,42 +127,48 @@
         )
 
     first_copy = remote(first.at[core], first.at[core], first_sem.at[0], first_sem.at[1], mate)
-    weight_copies = [
+    held_copy = remote(held.at[0, 0], held.at[0, 0], held_sem.at[0], held_sem.at[1], mate)
+
+    def swap_copy(index):
+        stage = stages[index]
+        if len(stage) == 2:
+            source, target = transfer.at[stage[1], :, side(1 - core)], foreign.at[index, :, pl.ds(0, rank)]
+        else:
+            source, target = transfer.at[stage[0]], foreign.at[index]
+        return remote(source, target, weight_sem.at[index, 0], weight_sem.at[index, 1], mate)
+
+    def mixing_copy(index, outer):
+        part = mixing.at[index, :, pl.ds(0, rank), pl.ds(outer * rank, rank)]
+        return remote(part, part, weight_sem.at[index, 2 + outer], weight_sem.at[index, 4 + outer], mate)
+
+    def stage_start(index, which, piece):
         remote(
-            transfer.at[1 + index], foreign.at[index], weight_send.at[index], weight_recv.at[index], mate
-        )
-        for index in range(levels - 2)
-    ]
-    held_copy = remote(held.at[0, 0], held.at[0, 0], held_sem.at[0], held_sem.at[1], mate)
-
-    def stage_copy(index, which, piece):
-        return remote(
             held.at[index, which, spans[piece]], arrived.at[index, which, spans[piece]],
-            stage_send.at[index, which, piece], stage_recv.at[index, which, piece],
-            across(stages[index][0], 1),
-        )
+            stage_send.at[index], stage_recv.at[index, piece], across(stages[index][0], 1),
+        ).start()
+
+    def stage_arrival(index, piece):
+        both = arrived.at[index, :, spans[piece]]
+        return remote(both, both, stage_send.at[index], stage_recv.at[index, piece], mate)
 
     mine = bit_of(final)
 
     def last_copy(which, piece):
         source = lent.at[spans[piece]] if which == 0 else last.at[mine, spans[piece]]
         return remote(
-            source, last.at[mine, spans[piece]], last_send.at[which, piece], last_recv.at[piece],
-            across(final, which),
+            source, last.at[mine, spans[piece]], last_send.at[which], last_recv.at[piece], across(final, which)
         )
 
-    def down_copy(piece):
-        return remote(
-            lent.at[spans[piece]], last.at[mine, spans[piece]], down_send.at[piece],
-            down_recv.at[piece], mate,
-        )
+    def down_copy(span):
+        return remote(lent.at[span], last.at[mine, span], down_sem.at[0], down_sem.at[1], mate)
 
     def scatter_copy(piece, slot):
         return remote(
-            outgoing.at[piece, slot], incoming.at[piece, slot],
-            scatter_send.at[piece, slot], scatter_recv.at[piece, slot],
+            outgoing.at[piece, slot], incoming.at[piece, slot], scatter_send.at[0], scatter_recv.at[piece],
             {"blk": block ^ (n_blk - 1 - slot)},
         )
+
+    everything, others = pl.ds(0, count), pl.ds(0, n_blk - 1)
 
     def scatter(piece, target, held_back):
         far = (block >= n_blk // 2) if n_blk // 4 <= target < n_blk // 2 else None
@@ -192,13 +195,16 @@
         value = last[1 - mine, spans[piece], :]
         return contract(merged[:, side(1 - mine)], jnp.concatenate([value] * pieces, axis=0))
 
-    def weights(level, which):
-        return transfer.at[level] if which else foreign.at[level - 1]
-
-    def turn(level, inner):
+    def turn(index):
+        level = stages[index][0]
         bit = bit_of(level)
         for half, which in ((0, bit), (1, 1 - bit)):
-            turned[inner, half * rank : (half + 1) * rank] = weights(level, inner)[:, side(which)].T
+            turned[half * rank : (half + 1) * rank] = transfer[level, :, side(which)].T
+
+    def join(index, outer, factor):
+        both = contract(turned[...], factor).astype(BF16)
+        for half in range(2):
+            mixing[index, half, side(core), side(outer)] = both[half * rank : (half + 1) * rank]
 
     loads[0].wait()
     loads[1].wait()
@@ -209,80 +215,73 @@
     first_copy.start()
     for level in range(final):
         transfer_loads[level].wait()
-
-    @pl.when(helper)
-    def _():
-        for copy in weight_copies:
-            copy.start()
-
+    for index, stage in enumerate(stages):
+        if len(stage) == 2:
+            swap_copy(index).start()
     own = contract(first[core], transfer[0, :, side(core)])
-    transfer_loads[final].wait()
-    for copy in row_loads:
-        copy.wait()
-    merged[...] = jnp.dot(row[...], transfer[final], preferred_element_type=F32).astype(BF16)
-
-    @pl.when(host)
-    def _():
-        if len(stages[0]) == 2:
-            turn(entry, 1)
-
+    if len(stages[0]) == 2:
+        turn(0)
+        join(0, core, transfer[stages[0][1], :, side(core)])
     first_copy.wait_recv()
     state = own + contract(first[1 - core], transfer[0, :, side(1 - core)])
     held[0, core] = state.astype(BF16)
     for piece in range(pieces):
-        stage_copy(0, core, piece).start()
+        stage_start(0, core, piece)
+
+    @pl.when(helper)
+    def _():
+        held_copy.start()
+        for index, stage in enumerate(stages):
+            if len(stage) == 1:
+                swap_copy(index).start()
+            elif index == 0:
+                mixing_copy(index, 0).start()
+
     hear(0)
     tell(1)
+    for index, stage in enumerate(stages):
+        if len(stage) == 2:
+            if index:
+                turn(index)
+                join(index, core, transfer[stage[1], :, side(core)])
+            swap_copy(index).wait_recv()
+            join(index, 1 - core, foreign[index, :, :rank])
+
+            @pl.when(helper)
+            def _():
+                for outer in range(0 if index else 1, 2):
+                    mixing_copy(index, outer).start()
+
+    transfer_loads[final].wait()
+    whole = pltpu.make_async_copy(row, row, load_sem.at[levels + 2])
+    whole.wait()
+    merged[...] = jnp.dot(row[...], transfer[final], preferred_element_type=F32).astype(BF16)
 
     @pl.when(helper)
     def _():
-        held_copy.start()
-        for piece in range(pieces):
-            down_copy(piece).wait_recv()
-        own_rows()
-
-    def mix(index, states, incoming_side):
+        down_copy(everything).wait_recv()
+
+    def mix(index, states, arriving):
         stage = stages[index]
         if len(stage) == 2:
-            joined = jnp.concatenate(states, axis=1)
-            return jnp.dot(joined, mixing[incoming_side], preferred_element_type=F32)
-        which = bit_of(stage[0]) if incoming_side == 0 else 1 - bit_of(stage[0])
-        return jnp.concatenate(
-            [contract(states[c], weights(stage[0], c)[:, side(which)]) for c in range(2)], axis=1
-        )
-
-    def join(low, high, inner, outer):
-        both = contract(turned[inner], weights(high, outer)[:, inner * rank : (inner + 1) * rank])
-        for half in range(2):
-            mixing[half, inner * rank : (inner + 1) * rank, outer * rank : (outer + 1) * rank] = both[
-                half * rank : (half + 1) * rank
-            ].astype(BF16)
-
-    def prepare(stage):
-        low, high = stage
-        join(low, high, 1, 1)
-        weight_copies[low - 1].wait_recv()
-        turn(low, 0)
-        join(low, high, 0, 1)
-        weight_copies[high - 1].wait_recv()
-        join(low, high, 1, 0)
-        join(low, high, 0, 0)
+            return jnp.dot(jnp.concatenate(states, axis=1), mixing[index, arriving], preferred_element_type=F32)
+        bit = bit_of(stage[0])
+        which = side(1 - bit if arriving else bit)
+        factors = [foreign[index, :, which], transfer[stage[0], :, which]]
+        return jnp.concatenate([contract(*pair) for pair in zip(states, factors)], axis=1)
 
     @pl.when(host)
     def _():
+        held_copy.wait_recv()
         for index, stage in enumerate(stages):
             if len(stage) == 2:
-                if index:
-                    turn(stage[0], 1)
-                prepare(stage)
+                mixing_copy(index, 0).wait_recv()
+                mixing_copy(index, 1).wait_recv()
             else:
-                weight_copies[stage[0] - 1].wait_recv()
-            if index == 0:
-                held_copy.wait_recv()
+                swap_copy(index).wait_recv()
             begun[...] = mix(index, [held[index, 0], held[index, 1]], 0)
             for piece in range(pieces):
-                for which in range(2):
-                    stage_copy(index, which, piece).wait_recv()
+                stage_arrival(index, piece).wait_recv()
                 total = begun[spans[piece], :] + mix(
                     index, [arrived[index, 0, spans[piece], :], arrived[index, 1, spans[piece], :]], 1
                 )
@@ -290,15 +289,15 @@
                 if index + 1 < len(stages):
                     for which in range(2):
                         held[index + 1, which, spans[piece], :] = total[:, which * rank : (which + 1) * rank]
-                        stage_copy(index + 1, which, piece).start()
+                        stage_start(index + 1, which, piece)
                 else:
                     lent[spans[piece], :] = total[:, :rank]
                     last_copy(0, piece).start()
                     last[mine, spans[piece], :] = total[:, rank:]
                     last_copy(1, piece).start()
-                    down_copy(piece).start()
-        own_rows()
-
+                    down_copy(spans[piece]).start()
+
+    own_rows()
     for hop in range(1, blk_bits - 1):
         hear(hop)
         tell(hop + 1)
@@ -327,35 +326,44 @@
         for target in range(n_blk // 4, n_blk // 2):
             scatter(piece, target, True)
 
+    def sent(index, which):
+        source = held.at[index, which] if index == 0 else held.at[index]
+        remote(source, source, stage_send.at[index], stage_recv.at[index, 0], mate).wait_send()
+
     first_copy.wait_send()
-    for piece in range(pieces):
-        stage_copy(0, core, piece).wait_send()
+    sent(0, core)
+    for index, stage in enumerate(stages):
+        if len(stage) == 2:
+            swap_copy(index).wait_send()
 
     @pl.when(helper)
     def _():
         held_copy.wait_send()
-        for copy in weight_copies:
-            copy.wait_send()
+        for index, stage in enumerate(stages):
+            if len(stage) == 1:
+                swap_copy(index).wait_send()
+            else:
+                mixing_copy(index, 0).wait_send()
+                mixing_copy(index, 1).wait_send()
 
     @pl.when(host)
     def _():
-        for piece in range(pieces):
-            for index in range(1, len(stages)):
-                for which in range(2):
-                    stage_copy(index, which, piece).wait_send()
-            last_copy(0, piece).wait_send()
-            last_copy(1, piece).wait_send()
-            down_copy(piece).wait_send()
+        for index in range(1, len(stages)):
+            sent(index, 0)
+        for which in range(2):
+            whole = last.at[mine]
+            remote(whole, whole, last_send.at[which], last_recv.at[0], mate).wait_send()
+        down_copy(everything).wait_send()
 
     sums = []
     for piece in range(pieces):
         if piece == pieces - 1:
-            for other in range(pieces):
-                for slot in range(n_blk - 1):
-                    scatter_copy(other, slot).wait_send()
+            whole = outgoing.at[:, others]
+            remote(whole, whole, scatter_send.at[0], scatter_recv.at[0], mate).wait_send()
+        whole = incoming.at[piece, others]
+        remote(whole, whole, scatter_send.at[0], scatter_recv.at[piece], mate).wait_recv()
         total = outgoing[piece, n_blk - 1].astype(F32)
         for slot in range(n_blk - 2, -1, -1):
-            scatter_copy(piece, slot).wait_recv()
             total = total + incoming[piece, slot].astype(F32)
         sums.append(total * (1.0 / math.sqrt(n_blk)))
     for g in range(pieces):
@@ -374,7 +382,7 @@
         levels = transfer.shape[1]
         rows = row_leaf.shape[2]
         owned = rows // n_blk
-        _, stages = plan(levels, n_bfly.bit_length() - 1)
+        depth = len(plan(levels, n_bfly.bit_length() - 1)[1])
         assert n_blk & (n_blk - 1) == 0
         dma = pltpu.SemaphoreType.DMA
         return pl.pallas_call(
@@ -386,35 +394,32 @@
                 pltpu.VMEM((leaf, ports), BF16),
                 pltpu.VMEM((rank, leaf), BF16),
                 pltpu.VMEM((levels, rank, 2 * rank), BF16),
-                pltpu.VMEM((levels - 2, rank, 2 * rank), BF16),
+                pltpu.VMEM((depth, rank, 2 * rank), BF16),
                 pltpu.VMEM((rows, rank), BF16),
                 pltpu.VMEM((2, ports, rank), BF16),
-                pltpu.VMEM((len(stages), 2, ports, rank), BF16),
-                pltpu.VMEM((len(stages), 2, ports, rank), BF16),
+                pltpu.VMEM((depth, 2, ports, rank), BF16),
+                pltpu.VMEM((depth, 2, ports, rank), BF16),
                 pltpu.VMEM((ports, 2 * rank), F32),
-                pltpu.VMEM((2, 2 * rank, rank), BF16),
-                pltpu.VMEM((2, 2 * rank, 2 * rank), BF16),
+                pltpu.VMEM((2 * rank, rank), BF16),
+                pltpu.VMEM((depth, 2, 2 * rank, 2 * rank), BF16),
                 pltpu.VMEM((ports, rank), BF16),
                 pltpu.VMEM((2, ports, rank), BF16),
                 pltpu.VMEM((PIECES, n_blk, owned // PIECES, ports), BF16),
                 pltpu.VMEM((PIECES, n_blk, owned // PIECES, ports), BF16),
                 pltpu.VMEM((rows, 2 * rank), BF16),
                 pltpu.VMEM((rows, ports), F32),
-                dma((levels + 2,)),
-                dma((n_blk,)),
+                dma((levels + 3,)),
                 dma((2,)),
-                dma((levels - 2,)),
-                dma((levels - 2,)),
+                dma((depth, 6)),
                 dma((2,)),
-                dma((len(stages), 2, PIECES)),
-                dma((len(stages), 2, PIECES)),
-                dma((2, PIECES)),
+                dma((depth,)),
+                dma((depth, PIECES)),
+                dma((2,)),
                 dma((PIECES,)),
+                dma((2,)),
+                dma((1,)),
                 dma((PIECES,)),
-                dma((PIECES,)),
-                dma((PIECES, n_blk)),
-                dma((PIECES, n_blk)),
-                pltpu.SemaphoreType.REGULAR((n_blk.bit_length(), n_blk.bit_length())),
+                pltpu.SemaphoreType.REGULAR((max(1, n_blk.bit_length() - 2),)),
             ],
             compiler_params=pltpu.CompilerParams(collective_id=0, has_side_effects=True),
         )(port_vectors, column_leaf, transfer, row_leaf)

time: 21 us -> 20.3 us (0.967)
  Pallas kernels: 20.3 us -> 19.5 us
    pallas_call x1, Pallas kernels: 20.3 us -> 19.5 us  [local(): pl.pallas_call(functools.partial(kernel, n_blk, n_bfly, PIECES), out_shap...]
where the time goes in v4:
time: 20.3 us; the launch traced here: 20.1 us
  Pallas kernels  19.5 us (96%)
  local copies, waits for them, and re-layouts  0.61 us (3%)
    pallas_call x1, Pallas kernels, local(): pl.pallas_call(functools.partial(kernel, n_blk, n_bfly, PIECES), out_shap...  19.5 us
    unnamed x1, local copies, waits for them, and re-layouts  0.61 us

profile of v4, /device:TPU:0, one launch (start us, length us, event | category | flops | bytes accessed | tf_op | source)
XLA Modules:
  0.0 20.1 jit_solution(17009612462131245544)
XLA Ops:
  0.0 19.5 %shard_map.46 = bf16[1,96,128]{2,1,0:T(8,128)(2,1)S(1)} custom-call(bf16[1,1,768,128]{3,2,1,0:T(8,128)(2,1)} %ports_hbm.1, bf16[1,1,384,768]{3,2,1,0:T(8,128)(2,1)} %column_hbm.1, bf16[1,4,1,384,768]{4,3,2,1,0:T(8,128)(2,1)} %transfer_hbm.1, bf16[1,1,768,384]{3,2,1,0:T(8,128)(2,1)} %row_hbm.1), custom_call_target="tpu_custom_call" | custom-call | tf_op jit(solution)/shard_map/pallas_call | solution.py:388
  19.5 0.6 %copy.6 = bf16[1,96,128]{2,1,0:T(8,128)(2,1)} copy(bf16[1,96,128]{2,1,0:T(8,128)(2,1)S(1)} %shard_map.46) | data formatting | bytes 49152

commit v5 on v4

v5 whole, which is shorter than its diff:
```python
import functools
import math

import jax
import jax.numpy as jnp
from jax import lax
from jax.experimental import pallas as pl
from jax.experimental.pallas import tpu as pltpu
from jax.sharding import PartitionSpec as P

PIECES = 4
GROUPS = 2
MESH = pl.DeviceIdType.MESH
F32 = jnp.float32
BF16 = jnp.bfloat16


def plan(levels, bit_count):
    bits = [level % bit_count for level in range(levels)]
    stages, level = [], 1
    while level < levels - 1:
        assert bits[level] > 0
        pair = level + 1 < levels - 1 and bits[level + 1] == 0
        stages.append((level, level + 1) if pair else (level,))
        level += len(stages[-1])
    assert stages and bits[levels - 1] > 0
    return bits, stages


def contract(left, right):
    return lax.dot_general(left, right, (((1,), (1,)), ((), ())), preferred_element_type=F32)


def kernel(
    n_blk, n_bfly, pieces, groups,
    ports_hbm, column_hbm, transfer_hbm, row_hbm, out_ref,
    ports, column, transfer, foreign, upper, row, first, held, arrived, begun, turned, mixing, lent,
    last, outgoing, incoming, merged, partial,
    load_sem, first_sem, weight_sem, held_sem, stage_send, stage_recv, last_send, last_recv, down_sem,
    scatter_send, scatter_recv, meet_sem,
):
    levels, rank, _ = transfer.shape
    count = ports.shape[1]
    leaf = row.shape[0]
    owned = leaf // n_blk
    bits, stages = plan(levels, n_bfly.bit_length() - 1)
    entry, final = stages[0][0], levels - 1
    block = lax.axis_index("blk")
    position = lax.axis_index("bfly")
    core = lax.rem(position, 2)
    host, helper = core == 1, core == 0
    width = count // pieces
    spans = [pl.ds(piece * width, width) for piece in range(pieces)]
    tall, wide, quarter = owned // groups, count // groups, n_blk // 4

    def load(source, target, sem):
        copy = pltpu.make_async_copy(source, target, sem)
        copy.start()
        return copy

    loads = [
        load(ports_hbm.at[0, 0], ports, load_sem.at[levels]),
        load(column_hbm.at[0, 0], column, load_sem.at[levels + 1]),
    ]
    transfer_loads = {
        level: load(transfer_hbm.at[0, level, 0], transfer.at[level], load_sem.at[level])
        for level in range(levels)
    }
    row_load = load(row_hbm.at[0, 0], row, load_sem.at[levels + 2])

    def side(which):
        return pl.ds(pl.multiple_of(which * rank, rank), rank)

    def bit_of(level):
        return lax.rem(position // 2 ** bits[level], 2)

    def across(level, to_core):
        place = position + (1 - 2 * bit_of(level)) * 2 ** bits[level]
        return {"bfly": place - core + to_core}

    def near_peers(distance):
        pair = block // 2
        return [
            (pair >= 0, {"blk": block + 1 - 2 * lax.rem(block, 2)}),
            (pair >= distance, {"blk": block - 2 * distance}),
            (pair + distance < n_blk // 2, {"blk": block + 2 * distance}),
        ]

    def number(peers):
        return sum(there.astype(jnp.int32) for there, _ in peers)

    mate = {"bfly": position + 1 - 2 * core}
    barrier = pltpu.get_barrier_semaphore()

    def greet(target):
        pl.semaphore_signal(barrier, inc=1, device_id=target, device_id_type=MESH)

    host_bits = {}
    for level in [stage[0] for stage in stages] + [final]:
        host_bits.setdefault(bits[level], level)
    mixed_bits = {bits[final]: final, bits[entry]: entry}
    greet(mate)
    for level in mixed_bits.values():
        greet(across(level, 1 - core))

    @pl.when(host)
    def _():
        for level in host_bits.values():
            greet(across(level, 1))

    near = near_peers(1)
    for there, peer in near:
        pl.when(there)(functools.partial(greet, peer))

    turns = (n_blk // 2).bit_length() - 1

    def tell(turn):
        if turn < turns:
            for there, peer in near_peers(2**turn):

                @pl.when(there)
                def _(peer=peer):
                    pl.semaphore_signal(meet_sem.at[turn], inc=1, device_id=peer, device_id_type=MESH)

    def hear(turn):
        if turn < turns:
            pl.semaphore_wait(meet_sem.at[turn], number(near_peers(2**turn)))

    def remote(source, target, send_sem, recv_sem, device):
        return pltpu.make_async_remote_copy(
            src_ref=source, dst_ref=target, send_sem=send_sem, recv_sem=recv_sem,
            device_id=device, device_id_type=MESH,
        )

    first_copy = remote(first.at[core], first.at[core], first_sem.at[0], first_sem.at[1], mate)
    held_copy = remote(held.at[0, 0], held.at[0, 0], held_sem.at[0], held_sem.at[1], mate)

    def lower_copy(index):
        return remote(
            transfer.at[stages[index][0]], foreign.at[index], weight_sem.at[index, 0], weight_sem.at[index, 1], mate
        )

    def upper_copy(index):
        return remote(
            transfer.at[stages[index][1], :, pl.ds(rank, rank)], upper.at[index], weight_sem.at[index, 2],
            weight_sem.at[index, 3], mate,
        )

    def mixing_copy(index, half):
        part = mixing.at[index, half, pl.ds(0, rank), pl.ds(0, rank)]
        return remote(part, part, weight_sem.at[index, 4], weight_sem.at[index, 5 + half], mate)

    def stage_start(index, which, piece):
        remote(
            held.at[index, which, spans[piece]], arrived.at[index, which, spans[piece]],
            stage_send.at[index], stage_recv.at[index, piece], across(stages[index][0], 1),
        ).start()

    def stage_arrival(index, piece):
        both = arrived.at[index, :, spans[piece]]
        return remote(both, both, stage_send.at[index], stage_recv.at[index, piece], mate)

    mine = bit_of(final)

    def last_copy(which, piece):
        source = lent.at[spans[piece]] if which == 0 else last.at[mine, spans[piece]]
        return remote(
            source, last.at[mine, spans[piece]], last_send.at[which], last_recv.at[piece], across(final, which)
        )

    def down_copy(span):
        return remote(lent.at[span], last.at[mine, span], down_sem.at[0], down_sem.at[1], mate)

    everything, others = pl.ds(0, count), pl.ds(0, n_blk - 1)

    def scatter(part, target, late):
        ready = block != target
        if target >= quarter:
            far = block >= n_blk - quarter
            ready = jnp.logical_and(ready, far if late else jnp.logical_not(far))
        elif late:
            return

        @pl.when(ready)
        def _():
            remote(
                outgoing.at[part, target], incoming.at[part, block], scatter_send.at[0], scatter_recv.at[part],
                {"blk": target},
            ).start()

    def own_rows():
        value = contract(merged[:, side(mine)], last[mine])
        for start in range(0, leaf, tall):
            shift = start // tall % groups * wide
            rows = value[start : start + tall]
            partial[start : start + tall, :] = pltpu.roll(rows, shift, 1) if shift else rows

    def other_rows(part, first_row, end_row):
        value = last[1 - mine, part * wide : (part + 1) * wide, :]
        return contract(merged[first_row:end_row, side(1 - mine)], jnp.concatenate([value] * groups, axis=0))

    def turn(index, slot, matrix):
        bit = bit_of(stages[index][0])
        for half, which in ((0, bit), (1, 1 - bit)):
            turned[slot, half * rank : (half + 1) * rank] = matrix[:, side(which)].T

    def join(index, slot, inner, outer, factor):
        both = contract(turned[slot], factor).astype(BF16)
        for half in range(2):
            mixing[index, half, side(inner), side(outer)] = both[half * rank : (half + 1) * rank]

    def join_own(index):
        low, high = stages[index]
        turn(index, 0, transfer.at[low])
        join(index, 0, core, core, transfer[high, :, side(core)])

    def merge_rows():
        transfer_loads[final].wait()
        row_load.wait()
        merged[...] = jnp.dot(row[...], transfer[final], preferred_element_type=F32).astype(BF16)

    loads[0].wait()
    loads[1].wait()
    state = jnp.dot(column[...], ports[...], preferred_element_type=F32)
    first[core] = state.T.astype(BF16)
    pl.semaphore_wait(barrier, 1 + len(mixed_bits) + core * len(host_bits) + number(near))
    tell(0)
    first_copy.start()
    for level in range(final):
        transfer_loads[level].wait()

    @pl.when(helper)
    def _():
        lower_copy(0).start()

    own = contract(first[core], transfer[0, :, side(core)])
    if len(stages[0]) == 2:
        join_own(0)
    first_copy.wait_recv()
    state = own + contract(first[1 - core], transfer[0, :, side(1 - core)])
    held[0, core] = state.astype(BF16)
    for piece in range(pieces):
        stage_start(0, core, piece)
    @pl.when(helper)
    def _():
        held_copy.start()
        for index, stage in enumerate(stages):
            if index:
                lower_copy(index).start()
            if len(stage) == 2:
                upper_copy(index).start()
                if index:
                    join_own(index)
                for half in range(2):
                    mixing_copy(index, half).start()

    def mix(index, states, arriving):
        stage = stages[index]
        if len(stage) == 2:
            return jnp.dot(jnp.concatenate(states, axis=1), mixing[index, arriving], preferred_element_type=F32)
        bit = bit_of(stage[0])
        which = side(1 - bit if arriving else bit)
        factors = [foreign[index, :, which], transfer[stage[0], :, which]]
        return jnp.concatenate([contract(*pair) for pair in zip(states, factors)], axis=1)

    @pl.when(host)
    def _():
        for index, stage in enumerate(stages):
            if len(stage) == 2:
                if index:
                    join_own(index)
                lower_copy(index).wait_recv()
                turn(index, 1, foreign.at[index])
                join(index, 1, 0, 1, transfer[stage[1], :, :rank])
                upper_copy(index).wait_recv()
                join(index, 0, 1, 0, upper[index])
                mixing_copy(index, 0).wait_recv()
            else:
                lower_copy(index).wait_recv()
            if index == 0:
                held_copy.wait_recv()
            begun[...] = mix(index, [held[index, 0], held[index, 1]], 0)
            if index == 0:
                hear(0)
                tell(1)
            if len(stage) == 2:
                mixing_copy(index, 1).wait_recv()
            for piece in range(pieces):
                stage_arrival(index, piece).wait_recv()
                total = begun[spans[piece], :] + mix(
                    index, [arrived[index, 0, spans[piece], :], arrived[index, 1, spans[piece], :]], 1
                )
                total = total.astype(BF16)
                if index + 1 < len(stages):
                    for which in range(2):
                        held[index + 1, which, spans[piece], :] = total[:, which * rank : (which + 1) * rank]
                        stage_start(index + 1, which, piece)
                else:
                    lent[spans[piece], :] = total[:, :rank]
                    last_copy(0, piece).start()
                    last[mine, spans[piece], :] = total[:, rank:]
                    last_copy(1, piece).start()
                    down_copy(spans[piece]).start()


    @pl.when(helper)
    def _():
        merge_rows()
        hear(0)
        tell(1)
        down_copy(everything).wait_recv()

    @pl.when(host)
    def _():
        merge_rows()

    own_rows()

    for hop in range(1, turns):
        hear(hop)
        tell(hop + 1)
    lane = lax.broadcasted_iota(jnp.int32, (tall, count), 1)

    def choose(values):
        result = values[0]
        for k in range(1, groups):
            result = jnp.where(lane < k * wide, result, values[k])
        return result

    for part in range(groups):
        for piece in range(part * pieces // groups, (part + 1) * pieces // groups):
            last_copy(1, piece).wait_recv()
        for low, high in ((0, quarter), (quarter, n_blk)):
            total = partial[low * owned : high * owned, :] + other_rows(part, low * owned, high * owned)
            for target in range(low, high):
                top = (target - low) * owned
                packed = choose(
                    [
                        total[top + g * tall : top + (g + 1) * tall]
                        for g in ((k - part) % groups for k in range(groups))
                    ]
                )
                outgoing[part, target] = packed.astype(BF16)
                scatter(part, target, False)
        incoming[part, block] = outgoing[part, block]
    for part in range(groups):
        for target in range(quarter, n_blk):
            scatter(part, target, True)

    def sent(index, which):
        source = held.at[index, which] if index == 0 else held.at[index]
        remote(source, source, stage_send.at[index], stage_recv.at[index, 0], mate).wait_send()

    first_copy.wait_send()
    sent(0, core)

    @pl.when(helper)
    def _():
        held_copy.wait_send()
        for index, stage in enumerate(stages):
            lower_copy(index).wait_send()
            if len(stage) == 2:
                upper_copy(index).wait_send()
                part = mixing.at[index, :, pl.ds(0, rank), pl.ds(0, rank)]
                remote(part, part, weight_sem.at[index, 4], weight_sem.at[index, 5], mate).wait_send()

    @pl.when(host)
    def _():
        for index in range(1, len(stages)):
            sent(index, 0)
        for which in range(2):
            whole = last.at[mine]
            remote(whole, whole, last_send.at[which], last_recv.at[0], mate).wait_send()
        down_copy(everything).wait_send()

    sums = []
    for part in range(groups):
        if part == groups - 1:
            whole = outgoing.at[:, others]
            remote(whole, whole, scatter_send.at[0], scatter_recv.at[0], mate).wait_send()
        whole = incoming.at[part, others]
        remote(whole, whole, scatter_send.at[0], scatter_recv.at[part], mate).wait_recv()
        total = incoming[part, 0].astype(F32)
        for source in range(1, n_blk):
            total = total + incoming[part, source].astype(F32)
        sums.append(total * (1.0 / math.sqrt(n_blk)))
    for g in range(groups):
        value = choose([sums[(k - g) % groups] for k in range(groups)])
        if g:
            value = pltpu.roll(value, (count - g * wide) % count, 1)
        out_ref[0, g * tall : (g + 1) * tall, :] = value.astype(BF16)


def solution(mesh):
    n_blk, n_bfly = mesh.shape["blk"], mesh.shape["bfly"]

    def local(port_vectors, column_leaf, transfer, row_leaf):
        _, _, leaf, ports = port_vectors.shape
        rank = column_leaf.shape[2]
        levels = transfer.shape[1]
        rows = row_leaf.shape[2]
        owned = rows // n_blk
        depth = len(plan(levels, n_bfly.bit_length() - 1)[1])
        assert n_blk % 4 == 0 and n_blk & (n_blk - 1) == 0
        dma = pltpu.SemaphoreType.DMA
        return pl.pallas_call(
            functools.partial(kernel, n_blk, n_bfly, PIECES, GROUPS),
            out_shape=pltpu.VMEM((1, owned, ports), BF16),
            in_specs=[pl.BlockSpec(memory_space=pl.ANY)] * 4,
            out_specs=pl.BlockSpec(memory_space=pltpu.VMEM),
            scratch_shapes=[
                pltpu.VMEM((leaf, ports), BF16),
                pltpu.VMEM((rank, leaf), BF16),
                pltpu.VMEM((levels, rank, 2 * rank), BF16),
                pltpu.VMEM((depth, rank, 2 * rank), BF16),
                pltpu.VMEM((depth, rank, rank), BF16),
                pltpu.VMEM((rows, rank), BF16),
                pltpu.VMEM((2, ports, rank), BF16),
                pltpu.VMEM((depth, 2, ports, rank), BF16),
                pltpu.VMEM((depth, 2, ports, rank), BF16),
                pltpu.VMEM((ports, 2 * rank), F32),
                pltpu.VMEM((2, 2 * rank, rank), BF16),
                pltpu.VMEM((depth, 2, 2 * rank, 2 * rank), BF16),
                pltpu.VMEM((ports, rank), BF16),
                pltpu.VMEM((2, ports, rank), BF16),
                pltpu.VMEM((GROUPS, n_blk, owned // GROUPS, ports), BF16),
                pltpu.VMEM((GROUPS, n_blk, owned // GROUPS, ports), BF16),
                pltpu.VMEM((rows, 2 * rank), BF16),
                pltpu.VMEM((rows, ports), F32),
                dma((levels + 3,)),
                dma((2,)),
                dma((depth, 7)),
                dma((2,)),
                dma((depth,)),
                dma((depth, PIECES)),
                dma((2,)),
                dma((PIECES,)),
                dma((2,)),
                dma((1,)),
                dma((GROUPS,)),
                pltpu.SemaphoreType.REGULAR((n_blk.bit_length(),)),
            ],
            compiler_params=pltpu.CompilerParams(collective_id=0, has_side_effects=True),
        )(port_vectors, column_leaf, transfer, row_leaf)

    placed = (
        P("blk", "bfly", None, None),
        P("blk", "bfly", None, None),
        P("blk", None, "bfly", None, None),
        P("blk", "bfly", None, None),
    )
    return jax.shard_map(
        local, mesh=mesh, in_specs=placed, out_specs=P("bfly", "blk", None), check_vma=False
    )
```

time: 20.3 us -> 19.3 us (0.951)
  Pallas kernels: 19.5 us -> 18.5 us
    pallas_call x1, Pallas kernels: 19.5 us -> 18.5 us  [local(): pl.pallas_call(functools.partial(kernel, n_blk, n_bfly, PIECES, GROUPS),...]
where the time goes in v5:
time: 19.3 us; the launch traced here: 19.1 us
  Pallas kernels  18.5 us (96%)
  local copies, waits for them, and re-layouts  0.61 us (3%)
    pallas_call x1, Pallas kernels, local(): pl.pallas_call(functools.partial(kernel, n_blk, n_bfly, PIECES, GROUPS),...  18.5 us
    unnamed x1, local copies, waits for them, and re-layouts  0.61 us

profile of v5, /device:TPU:0, one launch (start us, length us, event | category | flops | bytes accessed | tf_op | source)
XLA Modules:
  0.0 19.1 jit_solution(8206423735809961900)
XLA Ops:
  0.0 18.5 %shard_map.46 = bf16[1,96,128]{2,1,0:T(8,128)(2,1)S(1)} custom-call(bf16[1,1,768,128]{3,2,1,0:T(8,128)(2,1)} %ports_hbm.1, bf16[1,1,384,768]{3,2,1,0:T(8,128)(2,1)} %column_hbm.1, bf16[1,4,1,384,768]{4,3,2,1,0:T(8,128)(2,1)} %transfer_hbm.1, bf16[1,1,768,384]{3,2,1,0:T(8,128)(2,1)} %row_hbm.1), custom_call_target="tpu_custom_call" | custom-call | tf_op jit(solution)/shard_map/pallas_call | solution.py:406
  18.5 0.6 %copy.6 = bf16[1,96,128]{2,1,0:T(8,128)(2,1)} copy(bf16[1,96,128]{2,1,0:T(8,128)(2,1)S(1)} %shard_map.46) | data formatting | bytes 49152

commit v6 on v5

--- a/solution.py
+++ b/solution.py
@@ -176,7 +176,7 @@
     def scatter(part, target, late):
         ready = block != target
         if target >= quarter:
-            far = block >= n_blk - quarter
+            far = block >= quarter
             ready = jnp.logical_and(ready, far if late else jnp.logical_not(far))
         elif late:
             return
@@ -221,8 +221,8 @@
 
     loads[0].wait()
     loads[1].wait()
-    state = jnp.dot(column[...], ports[...], preferred_element_type=F32)
-    first[core] = state.T.astype(BF16)
+    state = lax.dot_general(ports[...], column[...], (((0,), (1,)), ((), ())), preferred_element_type=F32)
+    first[core] = state.astype(BF16)
     pl.semaphore_wait(barrier, 1 + len(mixed_bits) + core * len(host_bits) + number(near))
     tell(0)
     first_copy.start()
@@ -299,8 +299,9 @@
                     lent[spans[piece], :] = total[:, :rank]
                     last_copy(0, piece).start()
                     last[mine, spans[piece], :] = total[:, rank:]
-                    last_copy(1, piece).start()
                     down_copy(spans[piece]).start()
+        for piece in range(pieces):
+            last_copy(1, piece).start()
 
 
     @pl.when(helper)

time: 19.3 us -> 18.8 us (0.974)
  Pallas kernels: 18.5 us -> 18.1 us
    pallas_call x1, Pallas kernels: 18.5 us -> 18.1 us  [local(): pl.pallas_call(functools.partial(kernel, n_blk, n_bfly, PIECES, GROUPS),...]
where the time goes in v6:
time: 18.8 us; the launch traced here: 18.7 us
  Pallas kernels  18.1 us (96%)
  local copies, waits for them, and re-layouts  0.61 us (3%)
    pallas_call x1, Pallas kernels, local(): pl.pallas_call(functools.partial(kernel, n_blk, n_bfly, PIECES, GROUPS),...  18.1 us
    unnamed x1, local copies, waits for them, and re-layouts  0.61 us

profile of v6, /device:TPU:0, one launch (start us, length us, event | category | flops | bytes accessed | tf_op | source)
XLA Modules:
  0.0 18.7 jit_solution(2418661237603270201)
XLA Ops:
  0.0 18.1 %shard_map.46 = bf16[1,96,128]{2,1,0:T(8,128)(2,1)S(1)} custom-call(bf16[1,1,768,128]{3,2,1,0:T(8,128)(2,1)} %ports_hbm.1, bf16[1,1,384,768]{3,2,1,0:T(8,128)(2,1)} %column_hbm.1, bf16[1,4,1,384,768]{4,3,2,1,0:T(8,128)(2,1)} %transfer_hbm.1, bf16[1,1,768,384]{3,2,1,0:T(8,128)(2,1)} %row_hbm.1), custom_call_target="tpu_custom_call" | custom-call | tf_op jit(solution)/shard_map/pallas_call | solution.py:407
  18.1 0.6 %copy.6 = bf16[1,96,128]{2,1,0:T(8,128)(2,1)} copy(bf16[1,96,128]{2,1,0:T(8,128)(2,1)S(1)} %shard_map.46) | data formatting | bytes 49152

commit v7 on v6

--- a/solution.py
+++ b/solution.py
@@ -165,7 +165,8 @@
     def last_copy(which, piece):
         source = lent.at[spans[piece]] if which == 0 else last.at[mine, spans[piece]]
         return remote(
-            source, last.at[mine, spans[piece]], last_send.at[which], last_recv.at[piece], across(final, which)
+            source, last.at[mine, spans[piece]], last_send.at[which], last_recv.at[piece * groups // pieces],
+            across(final, which),
         )
 
     def down_copy(span):
@@ -329,8 +330,8 @@
         return result
 
     for part in range(groups):
-        for piece in range(part * pieces // groups, (part + 1) * pieces // groups):
-            last_copy(1, piece).wait_recv()
+        whole = last.at[1 - mine, pl.ds(part * wide, wide)]
+        remote(whole, whole, last_send.at[1], last_recv.at[part], mate).wait_recv()
         for low, high in ((0, quarter), (quarter, n_blk)):
             total = partial[low * owned : high * owned, :] + other_rows(part, low * owned, high * owned)
             for target in range(low, high):
@@ -435,11 +436,11 @@
                 dma((depth,)),
                 dma((depth, PIECES)),
                 dma((2,)),
-                dma((PIECES,)),
+                dma((GROUPS,)),
                 dma((2,)),
                 dma((1,)),
                 dma((GROUPS,)),
-                pltpu.SemaphoreType.REGULAR((n_blk.bit_length(),)),
+                pltpu.SemaphoreType.REGULAR((n_blk.bit_length() - 2,)),
             ],
             compiler_params=pltpu.CompilerParams(collective_id=0, has_side_effects=True),
         )(port_vectors, column_leaf, transfer, row_leaf)

time: 18.8 us -> 18.8 us (level)
  no operation moved by 1% of the time
where the time goes in v7:
time: 18.8 us; the launch traced here: 18.6 us
  Pallas kernels  18 us (96%)
  local copies, waits for them, and re-layouts  0.61 us (3%)
    pallas_call x1, Pallas kernels, local(): pl.pallas_call(functools.partial(kernel, n_blk, n_bfly, PIECES, GROUPS),...  18 us
    unnamed x1, local copies, waits for them, and re-layouts  0.61 us

profile of v7, /device:TPU:0, one launch (start us, length us, event | category | flops | bytes accessed | tf_op | source)
XLA Modules:
  0.0 18.6 jit_solution(1026370231891089293)
XLA Ops:
  0.0 18.0 %shard_map.46 = bf16[1,96,128]{2,1,0:T(8,128)(2,1)S(1)} custom-call(bf16[1,1,768,128]{3,2,1,0:T(8,128)(2,1)} %ports_hbm.1, bf16[1,1,384,768]{3,2,1,0:T(8,128)(2,1)} %column_hbm.1, bf16[1,4,1,384,768]{4,3,2,1,0:T(8,128)(2,1)} %transfer_hbm.1, bf16[1,1,768,384]{3,2,1,0:T(8,128)(2,1)} %row_hbm.1), custom_call_target="tpu_custom_call" | custom-call | tf_op jit(solution)/shard_map/pallas_call | solution.py:408
  18.0 0.6 %copy.6 = bf16[1,96,128]{2,1,0:T(8,128)(2,1)} copy(bf16[1,96,128]{2,1,0:T(8,128)(2,1)S(1)} %shard_map.46) | data formatting | bytes 49152
